TPU v7x, 128 devices: a whole 4x4x4 slice. The times are simulated.
128 devices in a mesh: fsdp: 8 (over x_lo, y), seq: 16 (over x_hi, z, core).
Axes of the slice: x: 4 (x_hi: 2, x_lo: 2; x = x_hi * 2 + x_lo), y: 4, z: 4, core: 2. Of those that a mesh axis runs over, the one named last changes fastest.
Arguments:
- image_input: bfloat16 [8, 2048, 1536], P('fsdp', 'seq'), may hold values from -6 to 6
- text_input: bfloat16 [8, 128, 1536], P('fsdp'), may hold values from -6 to 6
- w_qkv: bfloat16 [1536, 3, 2048], P('fsdp'), may hold values from -0.15625 to 0.15625
- query_gain: float32 [128], replicated, may hold values from 1.2 to 2.4
- key_gain: float32 [128], replicated, may hold values from 1.2 to 2.4
- image_cotangent: bfloat16 [8, 2048, 2048], P('fsdp', 'seq'), may hold values from -6 to 6
- text_cotangent: bfloat16 [8, 128, 2048], P('fsdp'), may hold values from -6 to 6
Outputs:
- image_grad: bfloat16 [8, 2048, 1536], P('fsdp', 'seq')
- text_grad: bfloat16 [8, 128, 1536], P('fsdp')
- weight_grad: float32 [1536, 3, 2048], P('fsdp', None, 'seq')
- gain_grad: float32 [2, 128], replicated
All inputs are finite; a program needn't handle non-finite values.
Results may differ from a plain program's by a relative error of at most 0.018.
The roundings to bfloat16 on the way count: a program that leaves them out, or rounds other values in their place, can miss the bound.
Values may be sent and summed in bfloat16 or wider, within the bound.
A program may use at most 192 MiB of HBM per device.

v0:
```python
import math
import jax
import jax.numpy as jnp
from jax import lax
from jax.sharding import Mesh
from jax.sharding import PartitionSpec as P

HEADS = 16
HEAD = 128
SEQ = ("seq_0", "seq_1", "seq_2")
FSDP = ("fsdp_0", "fsdp_1")
FSDP_SEQ = ("fsdp_0", "fsdp_1", "seq_0", "seq_1", "seq_2")
epsilon = 1e-06
query_parts = 4


def over_axes(shard, axes):
    for axis in axes:
        shard = lax.psum(shard, axis)
    return shard


def sent_to_all(shard, axis):
    copies = jnp.broadcast_to(shard, (lax.axis_size(axis), *shard.shape))
    return lax.all_to_all(copies, axis, split_axis=0, concat_axis=0, tiled=True)


def in_order(pieces, dim):
    pieces = jnp.moveaxis(pieces, 0, dim)
    lengths = pieces.shape
    return pieces.reshape(*lengths[:dim], lengths[dim] * lengths[dim + 1], *lengths[dim + 2 :])


def collect(shard, axis, dim):
    pieces = sent_to_all(shard, axis)
    return in_order(pieces, dim)


def rms_forward(values, gain):
    floated = values.astype(jnp.float32)
    inverse = lax.rsqrt(jnp.mean(floated * floated, axis=-1, keepdims=True) + epsilon)
    return (floated, inverse, (floated * inverse * gain).astype(jnp.bfloat16))


def rms_backward(floated, inverse, gain, incoming):
    weighted = incoming * gain
    inner_mean = jnp.mean(weighted * floated, axis=-1, keepdims=True)
    grad_input = inverse * weighted - floated * inverse * inverse * inverse * inner_mean
    grad_gain = jnp.sum(incoming * floated * inverse, axis=0)
    return (grad_input, grad_gain)


def head_backward(query_rows, key_rows, value_rows, incoming, query_gain, key_gain):
    query_float, query_inverse, query_normed = rms_forward(query_rows, query_gain)
    key_float, key_inverse, key_normed = rms_forward(key_rows, key_gain)
    length = query_rows.shape[0]
    width = query_rows.shape[1]
    block_rows = length // query_parts
    factor = 1.0 / math.sqrt(width)
    query_blocks = query_normed.reshape(query_parts, block_rows, width)
    incoming_blocks = incoming.reshape(query_parts, block_rows, width)

    def visit(carried, pieces):
        key_total, value_total = carried
        query_piece, incoming_piece = pieces
        scores = jnp.dot(query_piece, key_normed.T, preferred_element_type=jnp.float32) * factor
        attention = jax.nn.softmax(scores, axis=-1)
        attention_grad = jnp.dot(incoming_piece, value_rows.T, preferred_element_type=jnp.float32)
        row_dot = jnp.sum(attention * attention_grad, axis=-1, keepdims=True)
        score_grad = (attention * (attention_grad - row_dot)).astype(jnp.bfloat16)
        value_total = value_total + jnp.dot(
            attention.astype(jnp.bfloat16).T, incoming_piece, preferred_element_type=jnp.float32
        )
        key_total = (
            key_total
            + jnp.dot(score_grad.T, query_piece, preferred_element_type=jnp.float32) * factor
        )
        query_grad = jnp.dot(score_grad, key_normed, preferred_element_type=jnp.float32) * factor
        return ((key_total, value_total), query_grad)

    zeros_init = jnp.zeros((length, width), jnp.float32)
    (key_total, value_total), query_pieces = lax.scan(
        visit, (zeros_init, zeros_init), (query_blocks, incoming_blocks)
    )
    query_grad = query_pieces.reshape(length, width)
    query_input_grad, query_gain_grad = rms_backward(
        query_float, query_inverse, query_gain, query_grad
    )
    key_input_grad, key_gain_grad = rms_backward(key_float, key_inverse, key_gain, key_total)
    stacked = jnp.stack([query_input_grad, key_input_grad, value_total], axis=1).astype(
        jnp.bfloat16
    )
    return (stacked, jnp.stack([query_gain_grad, key_gain_grad], axis=0))


def local(image_input, text_input, w_qkv, query_gain, key_gain, image_cotangent, text_cotangent):
    member_count = lax.axis_size(SEQ)
    own_index = lax.axis_index(SEQ)
    local_heads = HEADS // member_count
    own_width = local_heads * HEAD
    offset = own_index * own_width
    text_length = text_input.shape[1]
    image_rows_dev = image_input.shape[1]
    weights = lax.all_gather(w_qkv, FSDP, axis=0, tiled=True)
    image_triple = jnp.einsum(
        "btd,dch->btch", image_input, weights, preferred_element_type=jnp.float32
    ).astype(jnp.bfloat16)
    stacked = jnp.concatenate([image_triple, image_cotangent[:, :, None, :]], axis=2)
    arrived = lax.all_to_all(stacked, SEQ, split_axis=3, concat_axis=1, tiled=True)
    own_weights = lax.dynamic_slice_in_dim(weights, offset, own_width, 2)
    text_triple = jnp.einsum(
        "btd,dch->btch", text_input, own_weights, preferred_element_type=jnp.float32
    ).astype(jnp.bfloat16)
    text_incoming = lax.dynamic_slice_in_dim(text_cotangent, offset, own_width, 2)
    joined_triple = jnp.concatenate([text_triple, arrived[:, :, :3]], axis=1)
    joined_incoming = jnp.concatenate([text_incoming, arrived[:, :, 3]], axis=1)
    batch_rows = joined_triple.shape[0]
    length = joined_triple.shape[1]
    split_triple = joined_triple.reshape(batch_rows, length, 3, local_heads, HEAD)
    split_incoming = joined_incoming.reshape(batch_rows, length, local_heads, HEAD)
    per_head = jax.vmap(head_backward, in_axes=(1, 1, 1, 1, None, None), out_axes=(2, 0))
    per_batch = jax.vmap(per_head, in_axes=(0, 0, 0, 0, None, None), out_axes=(0, 0))
    head_grads, gain_parts = per_batch(
        split_triple[:, :, 0],
        split_triple[:, :, 1],
        split_triple[:, :, 2],
        split_incoming,
        query_gain,
        key_gain,
    )
    head_grads = head_grads.reshape(batch_rows, length, 3, own_width)
    text_grads = head_grads[:, :text_length]
    image_grads = head_grads[:, text_length:]
    gain_total = over_axes(jnp.sum(gain_parts, axis=(0, 1)), FSDP_SEQ)
    image_tokens, text_share = (
        lax.all_to_all(image_grads, SEQ, split_axis=1, concat_axis=3, tiled=True),
        lax.all_to_all(text_grads, SEQ, split_axis=1, concat_axis=3, tiled=True),
    )
    text_piece = jnp.einsum(
        "btch,dch->btd", text_share, weights, preferred_element_type=jnp.float32
    ).astype(jnp.bfloat16)
    text_out = collect(text_piece, SEQ, 1)
    image_out = jnp.einsum(
        "btch,dch->btd", image_tokens, weights, preferred_element_type=jnp.float32
    ).astype(jnp.bfloat16)
    text_part = jnp.einsum(
        "btd,btch->dch", text_input, text_grads, preferred_element_type=jnp.float32
    )
    whole_image = lax.all_gather(image_input, SEQ, axis=1, tiled=True)

    def add_block(block, running):
        start = (block * image_rows_dev).astype(jnp.int32)
        image_block = lax.dynamic_slice_in_dim(whole_image, start, image_rows_dev, 1)
        grad_block = lax.dynamic_slice_in_dim(image_grads, start, image_rows_dev, 1)
        selected = (block == own_index).astype(jnp.float32)
        term = (
            jnp.einsum("btd,btch->dch", image_block, grad_block, preferred_element_type=jnp.float32)
            + text_part * selected
        )
        rounded = lax.optimization_barrier(term.astype(jnp.bfloat16))
        return running + rounded.astype(jnp.float32)

    start_total = jnp.zeros((image_input.shape[2], 3, own_width), jnp.float32)
    head_total = lax.fori_loop(0, member_count, add_block, start_total)
    grad_weights = lax.psum_scatter(
        head_total.astype(jnp.bfloat16), FSDP, scatter_dimension=0, tiled=True
    ).astype(jnp.float32)
    return (image_out, text_out, grad_weights, gain_total)


def solution(mesh):
    finer = Mesh(
        mesh.devices.reshape(2, 4, 2, 4, 2), ("fsdp_0", "fsdp_1", "seq_0", "seq_1", "seq_2")
    )
    return jax.shard_map(
        local,
        mesh=finer,
        in_specs=(
            P(FSDP, SEQ, None),
            P(FSDP, None, None),
            P(FSDP, None, None),
            P(),
            P(),
            P(FSDP, SEQ, None),
            P(FSDP, None, None),
        ),
        out_specs=(P(FSDP, SEQ, None), P(FSDP, None, None), P(FSDP, None, SEQ), P()),
        check_vma=False,
    )
```

profile of v0, /device:TPU:1, one launch (start us, length us, event | category | flops | bytes accessed | tf_op | source)
XLA Modules:
  0.0 568.3 jit_solution(10059944847568096801)
XLA Ops:
  8.8 194.9 %all-gather.3.cloned.1.call-done = bf16[1536,3,2048]{2,0,1:T(8,128)(2,1)} async-done(((bf16[192,3,2048]{2,0,1:T(8,128)(2,1)}), bf16[1536,3,2048]{2,0,1:T(8,128)(2,1)}) %all-gather.3.cloned.1.call-update) | async-done | bytes 18874384 | tf_op jit(solution)/shard_map/all_gather | solution.py:104
  203.7 9.0 %fusion.31 = bf16[1,128,3,2048]{3,1,2,0:T(8,128)(2,1)S(1)} fusion(bf16[1536,3,2048]{2,0,1:T(8,128)(2,1)} %all-gather.3.cloned.1.call-done, bf16[1,128,1536]{2,1,0:T(8,128)(2,1)S(1)} %copy-done.15), kind=kOutput, calls=%fused_computation.41 | convolution fusion | flops 2416705536 | bytes 20840448 | tf_op jit(solution)/shard_map/btd,dch->btch/dot_general | solution.py:105
  212.9 2.6 copy.49
  215.5 7.4 %all-to-all-start = ((bf16[1,128,4,2048]{1,2,0,3:T(4,128)(2,1)}), bf16[1,128,4,2048]{1,2,0,3:T(4,128)(2,1)}, u32[]{:S(2)}, u32[]{:S(2)}) async-start(bf16[1,128,4,2048]{1,2,0,3:T(4,128)(2,1)} %copy.49), calls=%async_computation | async-start | bytes 4194304 | tf_op jit(solution)/shard_map/all_to_all | solution.py:109
  225.9 29.6 %all-to-all-done = bf16[1,128,4,2048]{1,2,0,3:T(4,128)(2,1)} async-done(((bf16[1,128,4,2048]{1,2,0,3:T(4,128)(2,1)}), bf16[1,128,4,2048]{1,2,0,3:T(4,128)(2,1)}, u32[]{:S(2)}, u32[]{:S(2)}) %all-to-all-start) | async-done | bytes 2097184 | tf_op jit(solution)/shard_map/all_to_all | solution.py:109
  255.5 4.3 copy.80
  259.8 4.2 all_to_all.41
  268.2 2.9 copy.52
  281.7 71.7 %while.29 = (s32[]{:T(128)}, f32[1,1,2176,128]{3,2,1,0:T(8,128)S(1)}, f32[1,1,2176,128]{3,2,1,0:T(8,128)}, f32[4,1,1,544,128]{4,3,2,1,0:T(8,128)}, bf16[4,1,1,54...) while((s32[]{:T(128)}, ...), condition=%wide.region_6.7_spmd.clone, body=%wide.region_2.6_spmd.clone.sunk | while | flops 1535592832 | bytes 89573472 | solution.py:82
  286.7 4.8 fusion.106
  304.3 5.1 fusion.106
  322.4 5.2 fusion.106
  327.5 2.4 multiply_reduce_fusion.3
  340.4 5.1 fusion.106
  354.9 2.7 copy.70
  359.3 2.7 copy.59
  369.6 7.2 %all-to-all-start.2 = ((bf16[1,128,3,128]{3,2,0,1:T(4,128)(2,1)}), bf16[1,128,3,128]{3,2,0,1:T(4,128)(2,1)S(1)}, u32[]{:S(2)}, u32[]{:S(2)}) async-start(bf16[1,128,3,128]{3,2,0,1:T(4,128)(2,1)} %copy.65), calls=%async_computation.2 | async-start | bytes 262144 | tf_op jit(solution)/shard_map/all_to_all | solution.py:137
  379.3 5.1 all-to-all-done.2
  384.4 9.0 %fusion.34 = bf16[8,1536]{1,0:T(8,128)(2,1)S(1)} fusion(bf16[1536,3,2048]{2,0,1:T(8,128)(2,1)} %all-gather.3.cloned.1.call-done, bf16[1,128,3,128]{3,2,0,1:T(4,128)(2,1)S(1)} %all-to-all-done.2), kind=kOutput, calls=%fused_computation.46 | convolution fusion | flops 151007232 | bytes 18997248 | tf_op jit(solution)/shard_map/btch,dch->btd/dot_general | solution.py:139
  394.2 4.0 all-to-all-start.3
  398.6 2.5 copy.63
  401.1 6.9 %all-to-all-done.3 = bf16[16,1,8,1536]{3,2,1,0:T(8,128)(2,1)S(1)} async-done(((bf16[16,1,8,1536]{3,2,1,0:T(8,128)(2,1)}), bf16[16,1,8,1536]{3,2,1,0:T(8,128)(2,1)S(1)}, u32[]{:S(2)}, u32[]{:S(2)}) %all-to-all-start.3) | async-done | bytes 393248 | tf_op jit(solution)/shard_map/all_to_all | solution.py:25
  408.8 5.4 all-to-all-start.1
  414.3 87.6 %while.30 = (s32[]{:T(128)}, f32[1536,3,128]{2,0,1:T(8,128)}, bf16[1,2048,1536]{1,2,0:T(8,128)(2,1)}, bf16[1,2048,3,128]{1,3,2,0:T(8,128)(2,1)S(1)}, s32[]{:T(12...) while((s32[]{:T(128)}, f32[1536,3,128]{2,0,1:T(8,128)}, ...), condition=%wide.region_10.11_spmd.clone, body=%wide.region_9.10_spmd.clone.sunk | while | flops 154533888 | bytes 9930411 | solution.py:164
  420.5 3.3 select_add_fusion.2
  426.1 3.3 select_add_fusion.2
  431.7 3.3 select_add_fusion.2
  437.2 3.3 select_add_fusion.2
  442.8 3.3 select_add_fusion.2
  448.4 3.3 select_add_fusion.2
  454.0 3.3 select_add_fusion.2
  459.5 3.3 select_add_fusion.2
  465.1 3.3 select_add_fusion.2
  470.7 3.3 select_add_fusion.2
  476.3 3.3 select_add_fusion.2
  481.9 3.3 select_add_fusion.2
  487.4 3.3 select_add_fusion.2
  493.0 3.3 select_add_fusion.2
  498.6 3.3 select_add_fusion.2
  501.9 2.8 convert_element_type.211
  504.8 3.8 psum.35
  508.6 6.1 %psum.36 = f32[2,128]{1,0:T(2,128)S(1)} all-reduce(f32[2,128]{1,0:T(2,128)S(1)} %psum.35), channel_id=1, replica_groups=mesh['fsdp_0'=2,'fsdp_1'=4,'seq_0'=2,'seq_1'=4,'seq_2'=2] {'fsdp_1'}, use_global_device_ids=true, to_apply=%region_15.16 | all-reduce | flops 256 | bytes 2048 | tf_op jit(solution)/shard_map/psum | solution.py:19
  514.7 5.7 psum.37
  520.4 9.2 %psum.38 = f32[2,128]{1,0:T(2,128)S(1)} all-reduce(f32[2,128]{1,0:T(2,128)S(1)} %psum.37), channel_id=1, replica_groups=mesh['fsdp_0'=2,'fsdp_1'=4,'seq_0'=2,'seq_1'=4,'seq_2'=2] {'seq_1'}, use_global_device_ids=true, to_apply=%region_17.18 | all-reduce | flops 256 | bytes 2048 | tf_op jit(solution)/shard_map/psum | solution.py:19
  529.6 8.8 %psum.39 = f32[2,128]{1,0:T(2,128)} all-reduce(f32[2,128]{1,0:T(2,128)S(1)} %psum.38), channel_id=1, replica_groups=mesh['fsdp_0'=2,'fsdp_1'=4,'seq_0'=2,'seq_1'=4,'seq_2'=2] {'seq_2'}, use_global_device_ids=true, to_apply=%region_18.19 | all-reduce | flops 256 | bytes 2048 | tf_op jit(solution)/shard_map/psum | solution.py:19
  538.3 4.0 copy.81
  542.4 2.5 reshape.756
  545.0 13.5 %fusion.33 = bf16[1,128,1536]{2,1,0:T(8,128)(2,1)} fusion(bf16[128,3,2048]{2,0,1:T(8,128)(2,1)S(1)} %reshape.756, bf16[1536,3,2048]{2,0,1:T(8,128)(2,1)} %all-gather.3.cloned.1.call-done), kind=kOutput, calls=%fused_computation.44 | convolution fusion | flops 2416115712 | bytes 20840448 | tf_op jit(solution)/shard_map/btch,dch->btd/dot_general | solution.py:143
  (164 shorter events, 123.1 us)
Async XLA Ops:
  8.0 216.0 %copy-start = (bf16[1,128,2048]{2,1,0:T(8,128)(2,1)S(1)}, bf16[1,128,2048]{2,1,0:T(8,128)(2,1)}, u32[]{:S(2)}) copy-start(bf16[1,128,2048]{2,1,0:T(8,128)(2,1)} %param.17) | copy-start | bytes 1572868
  8.0 195.7 %copy-start.15 = (bf16[1,128,1536]{2,1,0:T(8,128)(2,1)S(1)}, bf16[1,128,1536]{2,1,0:T(8,128)(2,1)}, u32[]{:S(2)}) copy-start(bf16[1,128,1536]{2,1,0:T(8,128)(2,1)} %param.11) | copy-start | bytes 1179652
  8.0 195.7 %all-gather.3.cloned.1.call-start = ((), (), s32[]{:S(2)}) async-start(), calls=%async_computation.5 | async-start | bytes 21233664 | tf_op jit(solution)/shard_map/all_gather | solution.py:104
  8.8 203.9 %copy-start.21 = (bf16[1,128,2048]{2,1,0:T(8,128)(2,1)S(1)}, bf16[1,128,2048]{2,1,0:T(8,128)(2,1)}, u32[]{:S(2)}) copy-start(bf16[1,128,2048]{2,1,0:T(8,128)(2,1)} %param.16) | copy-start | bytes 1572868
  215.5 40.0 %all-to-all-start = ((bf16[1,128,4,2048]{1,2,0,3:T(4,128)(2,1)}), bf16[1,128,4,2048]{1,2,0,3:T(4,128)(2,1)}, u32[]{:S(2)}, u32[]{:S(2)}) async-start(bf16[1,128,4,2048]{1,2,0,3:T(4,128)(2,1)} %copy.49), calls=%async_computation | async-start | bytes 4194304 | tf_op jit(solution)/shard_map/all_to_all | solution.py:109
  222.9 1.2 copy-start.18
  222.9 191.3 %all-gather.5.cloned.1.call-start = ((), (), s32[]{:S(2)}) async-start(), calls=%async_computation.6 | async-start | bytes 6684672 | tf_op jit(solution)/shard_map/all_gather | solution.py:149
  264.0 1.4 slice-start
  265.8 2.2 copy-start.7
  268.0 3.1 copy-start.22
  274.2 5.1 copy-start.23
  283.7 2.2 copy-start.2
  286.7 4.8 copy-start.3
  286.7 4.8 copy-start.20
  295.4 2.4 copy-start.4
  301.4 2.2 copy-start.2
  304.3 5.2 copy-start.3
  304.3 5.2 copy-start.20
  313.4 2.4 copy-start.4
  319.4 2.2 copy-start.2
  322.3 5.2 copy-start.3
  322.4 5.2 copy-start.20
  331.5 2.4 copy-start.4
  337.4 2.2 copy-start.2
  340.4 5.2 copy-start.3
  340.4 5.2 copy-start.20
  349.5 2.4 copy-start.4
  354.9 2.7 copy-start.5
  359.3 5.0 copy-start.6
  366.2 1.2 copy-start.14
  367.4 0.8 copy-start.10
  367.4 1.3 copy-start.8
  367.8 0.8 copy-start.12
  367.8 9.0 %copy-start.19 = (bf16[1,128,1536]{2,1,0:T(8,128)(2,1)S(1)}, bf16[1,128,1536]{2,1,0:T(8,128)(2,1)}, u32[]{:S(2)}) copy-start(bf16[1,128,1536]{2,1,0:T(8,128)(2,1)} %param.12) | copy-start | bytes 1179652
  369.6 14.8 %all-to-all-start.2 = ((bf16[1,128,3,128]{3,2,0,1:T(4,128)(2,1)}), bf16[1,128,3,128]{3,2,0,1:T(4,128)(2,1)S(1)}, u32[]{:S(2)}, u32[]{:S(2)}) async-start(bf16[1,128,3,128]{3,2,0,1:T(4,128)(2,1)} %copy.65), calls=%async_computation.2 | async-start | bytes 262144 | tf_op jit(solution)/shard_map/all_to_all | solution.py:137
  384.4 13.8 %copy-start.13 = (bf16[1,2176,1,128]{1,3,2,0:T(8,128)(2,1)S(1)}, bf16[1,2176,1,128]{1,3,2,0:T(8,128)(2,1)}, u32[]{:S(2)}) copy-start(bf16[1,2176,1,128]{1,3,2,0:T(8,128)(2,1)} %copy-done.12) | copy-start | bytes 1671172
  393.4 4.8 copy-start.9
  393.4 4.8 copy-start.11
  394.2 13.9 %all-to-all-start.3 = ((bf16[16,1,8,1536]{3,2,1,0:T(8,128)(2,1)}), bf16[16,1,8,1536]{3,2,1,0:T(8,128)(2,1)S(1)}, u32[]{:S(2)}, u32[]{:S(2)}) async-start(bf16[16,1,8,1536]{3,2,1,0:T(8,128)(2,1)} %broadcast_in_dim.17), calls=%async_computation.3 | async-start | bytes 786432 | tf_op jit(solution)/shard_map/all_to_all | solution.py:25
  408.0 0.7 copy-start.16
  408.8 129.6 %all-to-all-start.1 = ((bf16[1,2048,3,128]{3,2,0,1:T(4,128)(2,1)}), bf16[1,2048,3,128]{3,2,0,1:T(4,128)(2,1)}, u32[]{:S(2)}, u32[]{:S(2)}) async-start(bf16[1,2048,3,128]{3,2,0,1:T(4,128)(2,1)} %copy.63), calls=%async_computation.1 | async-start | bytes 4194304 | tf_op jit(solution)/shard_map/all_to_all | solution.py:136
  414.2 144.3 %reduce-scatter.2.cloned.1.call-start = ((), (), s32[]{:S(2)}) async-start(), calls=%async_computation.7 | async-start | bytes 1327104 | tf_op jit(solution)/shard_map/reduce_scatter | solution.py:165
  544.9 15.2 %copy-start.17 = (bf16[16,1,8,1536]{3,2,1,0:T(8,128)(2,1)S(1)}, bf16[16,1,8,1536]{3,2,1,0:T(8,128)(2,1)}, u32[]{:S(2)}) copy-start(bf16[16,1,8,1536]{3,2,1,0:T(8,128)(2,1)} %copy-done.16) | copy-start | bytes 1179652
  544.9 15.9 %copy-start.1 = (bf16[1,128,2048]{2,1,0:T(8,128)(2,1)S(1)}, bf16[1,128,2048]{2,1,0:T(8,128)(2,1)}, u32[]{:S(2)}) copy-start(bf16[1,128,2048]{2,1,0:T(8,128)(2,1)} %param.17) | copy-start | bytes 1572868
Sparse Core Ops, SparseCore 0:
  10.5 193.1 all-gather.2
  504.9 33.6 reduce-scatter.1
Sparse Core Ops, SparseCore 1:
  226.2 74.2 all-gather.4
where the time goes:
time: 571 us; the launch traced here: 568 us
  waiting for transfers between devices  237 us (42%)
  matrix products  124 us (22%)
  other arithmetic  74.9 us (13%)
  local copies, waits for them, and re-layouts  58.3 us (10%)
  blocking collectives  33.6 us (6%)
  starting transfers between devices  24.2 us (4%)
  between operations  15.8 us (3%)
    all_gather x1, waiting for transfers between devices, local(): weights = lax.all_gather(w_qkv, FSDP, axis=0, tiled=True)  195 us
    add x16, other arithmetic, add_block(): return running + rounded.astype(jnp.float32)  50.8 us
    dot_general x16, matrix products, add_block(): jnp.einsum('btd,btch->dch', image_block, grad_block, preferred_element_ty...  36.6 us
    psum x5, blocking collectives, over_axes(): shard = lax.psum(shard, axis)  33.6 us
    all_to_all x1, waiting for transfers between devices, local(): lax.all_to_all(stacked, SEQ, split_axis=3, concat_axis=1, tiled=True)  29.6 us
    dot_general x4, matrix products, visit(): jnp.dot(attention.astype(jnp.bfloat16).T, incoming_piece, preferred_eleme...  20.2 us
    dot_general x1, matrix products, local(): jnp.einsum('btch,dch->btd', image_tokens, weights, preferred_element_type...  13.5 us
    unnamed x46, local copies, waits for them, and re-layouts  11.6 us
  transfers between devices with their start and end apart: 7, of which 4 were waited for; matrix products, arithmetic and copies ran while one was open for 40% of the time, Pallas kernels for 0%

commit v1 on v0

--- a/solution.py
+++ b/solution.py
@@ -101,7 +101,15 @@
     offset = own_index * own_width
     text_length = text_input.shape[1]
     image_rows_dev = image_input.shape[1]
-    weights = lax.all_gather(w_qkv, FSDP, axis=0, tiled=True)
+    weights = jnp.concatenate(
+        lax.all_to_all(
+            jnp.stack([w_qkv for _ in range(lax.axis_size(FSDP))], axis=0),
+            axis_name=FSDP,
+            split_axis=0,
+            concat_axis=0,
+        ),
+        0,
+    )
     image_triple = jnp.einsum(
         "btd,dch->btch", image_input, weights, preferred_element_type=jnp.float32
     ).astype(jnp.bfloat16)

time: 571 us -> 602 us (1.054)
  blocking collectives: 33.6 us -> 247 us
  waiting for transfers between devices: 237 us -> 41.7 us
  local copies, waits for them, and re-layouts: 58.3 us -> 76 us
  matrix products: 124 us -> 117 us
    all_to_all x0 -> x1, blocking collectives: none -> 214 us  [local(): lax.all_to_all(jnp.stack([w_qkv for _ in range(lax.axis_size(FSDP))], axi...]
    all_gather x1 -> x0, waiting for transfers between devices: 195 us -> none  [local(): weights = lax.all_gather(w_qkv, FSDP, axis=0, tiled=True)]
    all_to_all x0 -> x1, local copies, waits for them, and re-layouts: none -> 9.8 us  [local(): lax.all_to_all(jnp.stack([w_qkv for _ in range(lax.axis_size(FSDP))], axi...]
    dot_general x1, matrix products: 8.98 us -> 2.62 us  [local(): jnp.einsum('btd,dch->btch', image_input, weights, preferred_element_type=...]
    unnamed x46 -> x48, local copies, waits for them, and re-layouts: 11.6 us -> 15.5 us
  transfers between devices with their start and end apart: 7 -> 6, of which waited for: 4 -> 3; matrix products, arithmetic and copies ran while one was open for 40% -> 37% of each run, Pallas kernels for 0% -> 0%
where the time goes in v1:
time: 602 us; the launch traced here: 600 us
  blocking collectives  247 us (41%)
  matrix products  117 us (19%)
  local copies, waits for them, and re-layouts  76 us (13%)
  other arithmetic  75.1 us (12%)
  waiting for transfers between devices  41.7 us (7%)
  starting transfers between devices  27 us (4%)
  between operations  14.4 us (2%)
    all_to_all x1, blocking collectives, local(): lax.all_to_all(jnp.stack([w_qkv for _ in range(lax.axis_size(FSDP))], axi...  214 us
    add x16, other arithmetic, add_block(): return running + rounded.astype(jnp.float32)  50.9 us
    dot_general x16, matrix products, add_block(): jnp.einsum('btd,btch->dch', image_block, grad_block, preferred_element_ty...  36.6 us
    psum x5, blocking collectives, over_axes(): shard = lax.psum(shard, axis)  33.4 us
    all_to_all x1, waiting for transfers between devices, local(): lax.all_to_all(stacked, SEQ, split_axis=3, concat_axis=1, tiled=True)  29.6 us
    dot_general x4, matrix products, visit(): jnp.dot(attention.astype(jnp.bfloat16).T, incoming_piece, preferred_eleme...  20.2 us
    unnamed x48, local copies, waits for them, and re-layouts  15.5 us
    dot_general x1, matrix products, local(): jnp.einsum('btch,dch->btd', image_tokens, weights, preferred_element_type...  13.5 us
  transfers between devices with their start and end apart: 6, of which 3 were waited for; matrix products, arithmetic and copies ran while one was open for 37% of the time, Pallas kernels for 0%

profile of v1, /device:TPU:1, one launch (start us, length us, event | category | flops | bytes accessed | tf_op | source)
XLA Modules:
  0.0 599.6 jit_solution(14147137257216403380)
XLA Ops:
  7.2 4.4 stack.32
  11.6 214.0 %all_to_all.58 = bf16[8,192,3,2048]{3,1,2,0:T(8,128)(2,1)} all-to-all(bf16[8,192,3,2048]{3,1,2,0:T(8,128)(2,1)S(1)} %stack.32), channel_id=1, replica_groups=mesh['fsdp_0'=2,'fsdp_1'=4,'seq_0'=2,'seq_1'=4,'seq_2'=2] {'fsdp_0','fsd..., dimensions={0} | all-to-all | bytes 37748736 | tf_op jit(solution)/shard_map/all_to_all | solution.py:105
  225.6 9.8 %copy.49 = bf16[8,192,3,2048]{3,1,0,2:T(8,128)(2,1)S(1)} copy(bf16[8,192,3,2048]{3,1,2,0:T(8,128)(2,1)} %all_to_all.58) | data formatting | bytes 37748736 | tf_op jit(solution)/shard_map/all_to_all | solution.py:105
  235.4 2.6 fusion.31
  238.0 3.8 copy-done.4
  242.0 2.6 copy.50
  244.6 9.9 %all-to-all-start.1 = ((bf16[1,128,4,2048]{1,2,0,3:T(4,128)(2,1)}), bf16[1,128,4,2048]{1,2,0,3:T(4,128)(2,1)}, u32[]{:S(2)}, u32[]{:S(2)}) async-start(bf16[1,128,4,2048]{1,2,0,3:T(4,128)(2,1)} %copy.50), calls=%async_computation.1 | async-start | bytes 4194304 | tf_op jit(solution)/shard_map/all_to_all | solution.py:117
  257.5 29.6 %all-to-all-done.1 = bf16[1,128,4,2048]{1,2,0,3:T(4,128)(2,1)} async-done(((bf16[1,128,4,2048]{1,2,0,3:T(4,128)(2,1)}), bf16[1,128,4,2048]{1,2,0,3:T(4,128)(2,1)}, u32[]{:S(2)}, u32[]{:S(2)}) %all-to-all-start.1) | async-done | bytes 2097184 | tf_op jit(solution)/shard_map/all_to_all | solution.py:117
  287.1 4.3 copy.81
  291.4 4.2 all_to_all.45
  299.8 2.8 copy.53
  313.3 71.6 %while.29 = (s32[]{:T(128)}, f32[1,1,2176,128]{3,2,1,0:T(8,128)S(1)}, f32[1,1,2176,128]{3,2,1,0:T(8,128)}, f32[4,1,1,544,128]{4,3,2,1,0:T(8,128)}, bf16[4,1,1,54...) while((s32[]{:T(128)}, ...), condition=%wide.region_6.7_spmd.clone, body=%wide.region_2.6_spmd.clone.sunk | while | flops 1535592832 | bytes 89573472 | solution.py:82
  318.3 4.8 fusion.106
  335.9 5.1 fusion.106
  353.9 5.1 fusion.106
  371.9 5.1 fusion.106
  386.4 2.7 copy.71
  390.8 2.7 copy.60
  401.1 7.6 %all-to-all-start.3 = ((bf16[1,128,3,128]{3,2,0,1:T(4,128)(2,1)}), bf16[1,128,3,128]{3,2,0,1:T(4,128)(2,1)S(1)}, u32[]{:S(2)}, u32[]{:S(2)}) async-start(bf16[1,128,3,128]{3,2,0,1:T(4,128)(2,1)} %copy.66), calls=%async_computation.3 | async-start | bytes 262144 | tf_op jit(solution)/shard_map/all_to_all | solution.py:145
  411.1 5.1 all-to-all-done.3
  416.2 9.0 %fusion.34 = bf16[8,1536]{1,0:T(8,128)(2,1)S(1)} fusion(bf16[1536,3,2048]{2,0,1:T(8,128)(2,1)} %bitcast.221, bf16[1,128,3,128]{3,2,0,1:T(4,128)(2,1)S(1)} %all-to-all-done.3), kind=kOutput, calls=%fused_computation.46 | convolution fusion | flops 151007232 | bytes 18997248 | tf_op jit(solution)/shard_map/btch,dch->btd/dot_general | solution.py:147
  426.0 4.0 all-to-all-start.4
  433.0 6.9 %all-to-all-done.4 = bf16[16,1,8,1536]{3,2,1,0:T(8,128)(2,1)S(1)} async-done(((bf16[16,1,8,1536]{3,2,1,0:T(8,128)(2,1)}), bf16[16,1,8,1536]{3,2,1,0:T(8,128)(2,1)S(1)}, u32[]{:S(2)}, u32[]{:S(2)}) %all-to-all-start.4) | async-done | bytes 393248 | tf_op jit(solution)/shard_map/all_to_all | solution.py:25
  440.6 5.4 all-to-all-start.2
  446.1 87.8 %while.30 = (s32[]{:T(128)}, f32[1536,3,128]{2,0,1:T(8,128)}, bf16[1,2048,1536]{1,2,0:T(8,128)(2,1)}, bf16[1,2048,3,128]{1,3,2,0:T(8,128)(2,1)S(1)}, s32[]{:T(12...) while((s32[]{:T(128)}, f32[1536,3,128]{2,0,1:T(8,128)}, ...), condition=%wide.region_10.11_spmd.clone, body=%wide.region_9.10_spmd.clone.sunk | while | flops 154533888 | bytes 9930411 | solution.py:172
  452.4 3.3 select_add_fusion.2
  457.9 3.3 select_add_fusion.2
  463.5 3.3 select_add_fusion.2
  469.1 3.3 select_add_fusion.2
  474.7 3.3 select_add_fusion.2
  480.3 3.3 select_add_fusion.2
  485.9 3.3 select_add_fusion.2
  491.5 3.3 select_add_fusion.2
  497.1 3.3 select_add_fusion.2
  502.7 3.3 select_add_fusion.2
  508.3 3.3 select_add_fusion.2
  513.8 3.3 select_add_fusion.2
  519.4 3.3 select_add_fusion.2
  525.0 3.3 select_add_fusion.2
  530.6 3.3 select_add_fusion.2
  533.9 2.8 convert_element_type.211
  536.8 3.8 psum.35
  540.6 6.1 %psum.36 = f32[2,128]{1,0:T(2,128)S(1)} all-reduce(f32[2,128]{1,0:T(2,128)S(1)} %psum.35), channel_id=1, replica_groups=mesh['fsdp_0'=2,'fsdp_1'=4,'seq_0'=2,'seq_1'=4,'seq_2'=2] {'fsdp_1'}, use_global_device_ids=true, to_apply=%region_15.16 | all-reduce | flops 256 | bytes 2048 | tf_op jit(solution)/shard_map/psum | solution.py:19
  546.7 5.7 psum.37
  552.4 9.0 %psum.38 = f32[2,128]{1,0:T(2,128)S(1)} all-reduce(f32[2,128]{1,0:T(2,128)S(1)} %psum.37), channel_id=1, replica_groups=mesh['fsdp_0'=2,'fsdp_1'=4,'seq_0'=2,'seq_1'=4,'seq_2'=2] {'seq_1'}, use_global_device_ids=true, to_apply=%region_17.18 | all-reduce | flops 256 | bytes 2048 | tf_op jit(solution)/shard_map/psum | solution.py:19
  561.4 8.8 %psum.39 = f32[2,128]{1,0:T(2,128)} all-reduce(f32[2,128]{1,0:T(2,128)S(1)} %psum.38), channel_id=1, replica_groups=mesh['fsdp_0'=2,'fsdp_1'=4,'seq_0'=2,'seq_1'=4,'seq_2'=2] {'seq_2'}, use_global_device_ids=true, to_apply=%region_18.19 | all-reduce | flops 256 | bytes 2048 | tf_op jit(solution)/shard_map/psum | solution.py:19
  570.2 4.0 copy.82
  576.8 13.5 %fusion.33 = bf16[1,128,1536]{2,1,0:T(8,128)(2,1)} fusion(bf16[128,3,2048]{2,0,1:T(8,128)(2,1)S(1)} %reshape.762, bf16[1536,3,2048]{2,0,1:T(8,128)(2,1)} %bitcast.222), kind=kOutput, calls=%fused_computation.44 | convolution fusion | flops 2416115712 | bytes 20840448 | tf_op jit(solution)/shard_map/btch,dch->btd/dot_general | solution.py:151
  (166 shorter events, 129.9 us)
Async XLA Ops:
  7.2 248.4 %copy-start = (bf16[1,128,2048]{2,1,0:T(8,128)(2,1)S(1)}, bf16[1,128,2048]{2,1,0:T(8,128)(2,1)}, u32[]{:S(2)}) copy-start(bf16[1,128,2048]{2,1,0:T(8,128)(2,1)} %param.17) | copy-start | bytes 1572868
  225.6 9.8 %copy-start.16 = (bf16[1,128,1536]{2,1,0:T(8,128)(2,1)S(1)}, bf16[1,128,1536]{2,1,0:T(8,128)(2,1)}, u32[]{:S(2)}) copy-start(bf16[1,128,1536]{2,1,0:T(8,128)(2,1)} %param.11) | copy-start | bytes 1179652
  235.4 6.4 %copy-start.4 = (bf16[8,192,3,2048]{3,1,0,2:T(8,128)(2,1)}, bf16[8,192,3,2048]{3,1,0,2:T(8,128)(2,1)S(1)}, u32[]{:S(2)}) copy-start(bf16[8,192,3,2048]{3,1,0,2:T(8,128)(2,1)S(1)} %copy.49) | copy-start | bytes 56623108
  235.4 6.4 %copy-start.22 = (bf16[1,128,2048]{2,1,0:T(8,128)(2,1)S(1)}, bf16[1,128,2048]{2,1,0:T(8,128)(2,1)}, u32[]{:S(2)}) copy-start(bf16[1,128,2048]{2,1,0:T(8,128)(2,1)} %param.16) | copy-start | bytes 1572868
  244.6 42.6 %all-to-all-start.1 = ((bf16[1,128,4,2048]{1,2,0,3:T(4,128)(2,1)}), bf16[1,128,4,2048]{1,2,0,3:T(4,128)(2,1)}, u32[]{:S(2)}, u32[]{:S(2)}) async-start(bf16[1,128,4,2048]{1,2,0,3:T(4,128)(2,1)} %copy.50), calls=%async_computation.1 | async-start | bytes 4194304 | tf_op jit(solution)/shard_map/all_to_all | solution.py:117
  254.5 1.2 copy-start.19
  254.5 191.6 %all-gather.2.cloned.1.call-start = ((), (), s32[]{:S(2)}) async-start(), calls=%async_computation.6 | async-start | bytes 6684672 | tf_op jit(solution)/shard_map/all_gather | solution.py:157
  295.6 1.4 slice-start
  297.4 2.2 copy-start.8
  299.6 3.0 copy-start.23
  305.7 5.1 copy-start.24
  315.3 2.2 copy-start.2
  318.3 4.8 copy-start.3
  318.3 4.8 copy-start.21
  327.0 2.4 copy-start.5
  332.9 2.2 copy-start.2
  335.9 5.2 copy-start.3
  335.9 5.2 copy-start.21
  345.0 2.4 copy-start.5
  351.0 2.2 copy-start.2
  353.9 5.2 copy-start.3
  353.9 5.2 copy-start.21
  363.0 2.4 copy-start.5
  368.9 2.2 copy-start.2
  371.9 5.2 copy-start.3
  371.9 5.2 copy-start.21
  381.0 2.4 copy-start.5
  386.4 2.7 copy-start.6
  390.8 5.0 copy-start.7
  397.7 1.2 copy-start.15
  398.9 0.8 copy-start.11
  398.9 1.3 copy-start.9
  399.3 0.8 copy-start.13
  399.3 9.4 %copy-start.20 = (bf16[1,128,1536]{2,1,0:T(8,128)(2,1)S(1)}, bf16[1,128,1536]{2,1,0:T(8,128)(2,1)}, u32[]{:S(2)}) copy-start(bf16[1,128,1536]{2,1,0:T(8,128)(2,1)} %param.12) | copy-start | bytes 1179652
  401.1 15.2 %all-to-all-start.3 = ((bf16[1,128,3,128]{3,2,0,1:T(4,128)(2,1)}), bf16[1,128,3,128]{3,2,0,1:T(4,128)(2,1)S(1)}, u32[]{:S(2)}, u32[]{:S(2)}) async-start(bf16[1,128,3,128]{3,2,0,1:T(4,128)(2,1)} %copy.66), calls=%async_computation.3 | async-start | bytes 262144 | tf_op jit(solution)/shard_map/all_to_all | solution.py:145
  416.2 13.8 %copy-start.14 = (bf16[1,2176,1,128]{1,3,2,0:T(8,128)(2,1)S(1)}, bf16[1,2176,1,128]{1,3,2,0:T(8,128)(2,1)}, u32[]{:S(2)}) copy-start(bf16[1,2176,1,128]{1,3,2,0:T(8,128)(2,1)} %copy-done.13) | copy-start | bytes 1671172
  425.2 4.8 copy-start.10
  425.2 4.8 copy-start.12
  426.0 13.9 %all-to-all-start.4 = ((bf16[16,1,8,1536]{3,2,1,0:T(8,128)(2,1)}), bf16[16,1,8,1536]{3,2,1,0:T(8,128)(2,1)S(1)}, u32[]{:S(2)}, u32[]{:S(2)}) async-start(bf16[16,1,8,1536]{3,2,1,0:T(8,128)(2,1)} %broadcast_in_dim.17), calls=%async_computation.4 | async-start | bytes 786432 | tf_op jit(solution)/shard_map/all_to_all | solution.py:25
  439.9 0.7 copy-start.17
  440.6 129.6 %all-to-all-start.2 = ((bf16[1,2048,3,128]{3,2,0,1:T(4,128)(2,1)}), bf16[1,2048,3,128]{3,2,0,1:T(4,128)(2,1)}, u32[]{:S(2)}, u32[]{:S(2)}) async-start(bf16[1,2048,3,128]{3,2,0,1:T(4,128)(2,1)} %copy.64), calls=%async_computation.2 | async-start | bytes 4194304 | tf_op jit(solution)/shard_map/all_to_all | solution.py:144
  446.0 144.3 %reduce-scatter.2.cloned.1.call-start = ((), (), s32[]{:S(2)}) async-start(), calls=%async_computation.7 | async-start | bytes 1327104 | tf_op jit(solution)/shard_map/reduce_scatter | solution.py:173
  576.8 15.2 %copy-start.18 = (bf16[16,1,8,1536]{3,2,1,0:T(8,128)(2,1)S(1)}, bf16[16,1,8,1536]{3,2,1,0:T(8,128)(2,1)}, u32[]{:S(2)}) copy-start(bf16[16,1,8,1536]{3,2,1,0:T(8,128)(2,1)} %copy-done.17) | copy-start | bytes 1179652
  576.8 15.9 %copy-start.1 = (bf16[1,128,2048]{2,1,0:T(8,128)(2,1)S(1)}, bf16[1,128,2048]{2,1,0:T(8,128)(2,1)}, u32[]{:S(2)}) copy-start(bf16[1,128,2048]{2,1,0:T(8,128)(2,1)} %param.17) | copy-start | bytes 1572868
Sparse Core Ops, SparseCore 0:
  258.2 74.0 all-gather.1
  536.9 33.4 reduce-scatter.1
